TPU v7x, 128 devices: a whole 4x4x4 slice. The times are simulated.
128 devices in a mesh: row: 8 (over z, x_lo), col: 16 (over y, x_hi, core).
Axes of the slice: x: 4 (x_hi: 2, x_lo: 2; x = x_hi * 2 + x_lo), y: 4, z: 4, core: 2. Of those that a mesh axis runs over, the one named last changes fastest.
Arguments:
- tokens: bfloat16 [256, 16384], P('row', 'col'), may hold values from -6 to 6
- probe_words: int32 [256, 512], P(None, 'col'), may hold values from -2147483648 to 2147483646, as said below
- token_ids: int32 [256], replicated, may hold values from 0 to 128255
- loss_weight: float32 [128256], replicated, may hold values from 0.5 to 2
- gate_weight: bfloat16 [16384, 26624], P('col', 'row'), may hold values from -0.046875 to 0.046875
- up_weight: bfloat16 [16384, 26624], P('col', 'row'), may hold values from -0.046875 to 0.046875
- down_weight: bfloat16 [26624, 16384], P('row', 'col'), may hold values from -0.0390625 to 0.0390625
Outputs:
- hvp: float32 [256, 16384], P('row', 'col')
Inputs may be any that keep to these rules, and one draw needn't show every extreme that they name: `probe_words`: every bit of every word is an independent fair sign bit; bit k of word j of token t is the probe sign of feature 32 j + k of that token (set: +1, clear: -1).
All inputs are finite; a program needn't handle non-finite values.
Results may differ from a plain program's by a relative error of at most 0.0036.
Values may be sent and summed in bfloat16 or wider, within the bound.
No kernel may reach another device: no remote copies, remote signals or barrier semaphores. Data moves between devices by JAX's collectives and lax.ppermute only.
A program may use at most 128 MiB of HBM per device.

v0:
```python
import jax
import jax.numpy as jnp
from jax import lax
from jax.sharding import PartitionSpec as P


def copy_for_each(x, axis):
    copies = jnp.broadcast_to(x, (lax.axis_size(axis), *x.shape))
    return lax.all_to_all(copies, axis, split_axis=0, concat_axis=0, tiled=True)


def laid_out(pieces, dim):
    dims = list(pieces.shape[1:])
    dims[dim] *= pieces.shape[0]
    return jnp.moveaxis(pieces, 0, dim).reshape(dims)


def gathered_copies(x, axis, dim):
    pieces = copy_for_each(x, axis)
    return laid_out(pieces, dim)


def side_by_side(arrays, axis, dim, along):
    both = jnp.concatenate(arrays, axis=along)
    result, at, finished = (lax.all_gather(both, axis, axis=dim, tiled=True), 0, [])
    for a in arrays:
        finished.append(lax.slice_in_dim(result, at, at + a.shape[along], axis=along))
        at += a.shape[along]
    return tuple(finished)


def in_blocks(x, dim, peers):
    before, after = (x.shape[:dim], x.shape[dim + 1 :])
    return jnp.moveaxis(x.reshape(*before, peers, -1, *after), dim, 0)


def summed_on_arrival(x, axis, dim):
    pieces = in_blocks(x, dim, lax.axis_size(axis))
    arrived = lax.all_to_all(pieces, axis, split_axis=0, concat_axis=0, tiled=True)
    return arrived.sum(axis=0)


def unpack_signs(packed):
    shifts = jnp.arange(32, dtype=jnp.int32)
    bit_vals = jnp.bitwise_and(jnp.right_shift(packed[:, :, None], shifts), 1)
    return (2 * bit_vals - 1).reshape(packed.shape[0], -1).astype(jnp.bfloat16)


def silu_parts(pre_act):
    sigmoid_pre = jax.nn.sigmoid(pre_act)
    active = pre_act * sigmoid_pre
    slopes = sigmoid_pre * (1.0 + pre_act * (1.0 - sigmoid_pre))
    curves = sigmoid_pre * (1.0 - sigmoid_pre) * (2.0 + pre_act * (1.0 - 2.0 * sigmoid_pre))
    return (active, slopes, curves)


def matmul(left_rows, weight):
    return jnp.dot(left_rows, weight, preferred_element_type=jnp.float32)


def matmul_trans(left_rows, weight):
    return lax.dot_general(
        left_rows, weight, (((1,), (1,)), ((), ())), preferred_element_type=jnp.float32
    )


def paired(first_rows, second_rows, weight, product):
    return (product(first_rows, weight), product(second_rows, weight))


def project_in(tok_rows, probe_rows, gate_weight, up_weight):
    gate_pre, gate_tan = paired(tok_rows, probe_rows, gate_weight, matmul)
    up_pre, up_tan = paired(tok_rows, probe_rows, up_weight, matmul)
    return (gate_pre, up_pre, gate_tan, up_tan)


def hidden_pair(gate_pre, up_pre, gate_tan, up_tan):
    active, slopes, curves = silu_parts(gate_pre)
    hidden = (active * up_pre).astype(jnp.bfloat16)
    hidden_tan = (slopes * gate_tan * up_pre + active * up_tan).astype(jnp.bfloat16)
    return (hidden, hidden_tan)


def back_pair(gate_pre, up_pre, gate_tan, up_tan, backward, back_tan):
    active, slopes, curves = silu_parts(gate_pre)
    gate_back = (
        back_tan * up_pre * slopes
        + backward * up_tan * slopes
        + backward * up_pre * curves * gate_tan
    ).astype(jnp.bfloat16)
    up_back = (back_tan * active + backward * slopes * gate_tan).astype(jnp.bfloat16)
    return (gate_back, up_back)


def on_device(tokens, probe_words, token_ids, loss_weight, gate_weight, up_weight, down_weight):
    gathered = gathered_copies(tokens, "row", 0)
    all_rows = gathered.shape[0]
    probe = unpack_signs(probe_words)
    hidden_width = gate_weight.shape[1]
    row_rows = all_rows // lax.axis_size("row")
    shares = lax.psum_scatter(
        jnp.concatenate(project_in(gathered, probe, gate_weight, up_weight), axis=1),
        "col",
        scatter_dimension=0,
        tiled=True,
    )
    gate_pre = shares[:, :hidden_width]
    up_pre = shares[:, hidden_width : 2 * hidden_width]
    gate_tan = shares[:, 2 * hidden_width : 3 * hidden_width]
    up_tan = shares[:, 3 * hidden_width :]
    hidden_share, tan_share = hidden_pair(gate_pre, up_pre, gate_tan, up_tan)
    hidden, hidden_tan = side_by_side((hidden_share, tan_share), "col", 0, 1)
    out_pieces = paired(hidden, hidden_tan, down_weight, matmul)
    output, out_tan = lax.psum((out_pieces[0], out_pieces[1]), "row")
    weight_tok = jnp.take(loss_weight, token_ids)[:, None]
    cotangent = (weight_tok * (gathered.astype(jnp.float32) + output)).astype(jnp.bfloat16)
    cot_tan = weight_tok * (probe.astype(jnp.float32) + out_tan)
    cot_half = cot_tan.astype(jnp.bfloat16)
    back_shares = lax.psum_scatter(
        jnp.concatenate(paired(cotangent, cot_half, down_weight, matmul_trans), axis=1),
        "col",
        scatter_dimension=0,
        tiled=True,
    )
    gate_share, up_share = back_pair(
        gate_pre,
        up_pre,
        gate_tan,
        up_tan,
        back_shares[:, :hidden_width],
        back_shares[:, hidden_width:],
    )
    gate_back, up_back = side_by_side((gate_share, up_share), "col", 0, 1)
    summed = summed_on_arrival(
        matmul_trans(gate_back, gate_weight) + matmul_trans(up_back, up_weight), "row", 0
    )
    own_tan = lax.dynamic_slice_in_dim(cot_tan, lax.axis_index("row") * row_rows, row_rows, 0)
    return own_tan + summed


def solution(mesh):
    return jax.shard_map(
        on_device,
        mesh=mesh,
        in_specs=(
            P("row", "col"),
            P(None, "col"),
            P(),
            P(),
            P("col", "row"),
            P("col", "row"),
            P("row", "col"),
        ),
        out_specs=P("row", "col"),
        check_vma=False,
    )
```

profile of v0, /device:TPU:0, one launch (start us, length us, event | category | flops | bytes accessed | tf_op | source)
XLA Modules:
  0.0 535.4 jit_solution(15537788906171822060)
XLA Ops:
  6.5 1.7 broadcast_in_dim.16
  8.3 6.4 %all-to-all-start = ((bf16[8,32,1024]{2,1,0:T(8,128)(2,1)}), bf16[8,32,1024]{2,1,0:T(8,128)(2,1)S(1)}, u32[]{:S(2)}, u32[]{:S(2)}) async-start(bf16[8,32,1024]{2,1,0:T(8,128)(2,1)} %broadcast_in_dim.16), calls=%async_computation | async-start | bytes 1048576 | tf_op jit(solution)/shard_map/all_to_all | solution.py:9
  14.7 0.8 shift_right_arithmetic.20
  15.5 0.3 copy.9
  15.9 6.7 %fusion.25 = f32[256,3328]{1,0:T(8,128)} fusion(bf16[1024,3328]{1,0:T(8,128)(2,1)} %param.11, s32[256,1024]{1,0:T(8,128)S(1)} %copy.9, s32[1024]{0:T(1024)S(1)} %shift_right_arithmetic.23), kind=kOutput, calls=%fused_computation.41 | convolution fusion | flops 1746141184 | bytes 11276288 | tf_op jit(solution)/shard_map/dot_general | solution.py:58
  22.6 6.6 %fusion.26 = f32[256,3328]{1,0:T(8,128)} fusion(bf16[1024,3328]{1,0:T(8,128)(2,1)} %param.12, s32[256,1024]{1,0:T(8,128)S(1)} %copy.9, s32[1024]{0:T(1024)S(1)} %shift_right_arithmetic.23), kind=kOutput, calls=%fused_computation.42 | convolution fusion | flops 1746141184 | bytes 11276288 | tf_op jit(solution)/shard_map/dot_general | solution.py:58
  29.3 5.0 fusion.23
  34.3 2.0 fusion.24
  36.3 1.0 copy-done.2
  37.3 5.1 pad_maximum_fusion
  42.5 128.6 %reduce-scatter.3.cloned.1.call-done = f32[16,13312]{1,0:T(8,128)} async-done(((f32[256,13312]{1,0:T(8,128)}), f32[16,13312]{1,0:T(8,128)}) %reduce-scatter.3.cloned.1.call-update) | async-done | bytes 851984 | tf_op jit(solution)/shard_map/reduce_scatter | solution.py:101
  171.1 1.4 multiply_convert_fusion.2
  172.5 0.7 pad_maximum_fusion.2
  173.3 50.1 %all-gather.3.cloned.1.call-done = bf16[256,6656]{1,0:T(8,128)(2,1)} async-done(((bf16[16,6656]{1,0:T(8,128)(2,1)}), bf16[256,6656]{1,0:T(8,128)(2,1)}) %all-gather.3.cloned.1.call-update) | async-done | bytes 3407888 | tf_op jit(solution)/shard_map/all_gather | solution.py:25
  223.4 6.5 %fusion.4 = f32[256,1024]{1,0:T(8,128)} fusion(bf16[3328,1024]{1,0:T(8,128)(2,1)} %param.13, bf16[256,6656]{1,0:T(8,128)(2,1)} %all-gather.3.cloned.1.call-done), kind=kOutput, calls=%fused_computation.7 | convolution fusion | flops 1744830464 | bytes 9568256 | tf_op jit(solution)/shard_map/dot_general | solution.py:58
  229.9 6.0 %fusion.6 = f32[256,1024]{1,0:T(8,128)} fusion(bf16[3328,1024]{1,0:T(8,128)(2,1)} %param.13, bf16[256,6656]{1,0:T(8,128)(2,1)S(1)} %copy-done.6), kind=kOutput, calls=%fused_computation.9 | convolution fusion | flops 1744830464 | bytes 9568256 | tf_op jit(solution)/shard_map/dot_general | solution.py:58
  235.9 0.2 reduce-scatter.5.cloned.1.call-start
  236.2 1.7 gather_fusion
  238.0 101.8 %all-reduce.3.cloned.1.call-done = (f32[256,1024]{1,0:T(8,128)}, f32[256,1024]{1,0:T(8,128)}) async-done(((f32[256,1024]{1,0:T(8,128)}, f32[256,1024]{1,0:T(8,128)}), (f32[256,1024]{1,0:T(8,128)}, f32[256,1024]{1,0:T(8,128)})) %all-reduce.3.cloned.1.call-update) | async-done | bytes 2097168 | tf_op jit(solution)/shard_map/psum | solution.py:114
  339.8 1.6 add_multiply_fusion
  341.5 5.1 fusion.12
  346.6 2.1 fusion.11
  348.7 3.6 pad_maximum_fusion.1
  352.4 91.2 %reduce-scatter.5.cloned.1.call-done = f32[16,6656]{1,0:T(8,128)} async-done(((f32[256,6656]{1,0:T(8,128)}), f32[16,6656]{1,0:T(8,128)}) %reduce-scatter.5.cloned.1.call-update) | async-done | bytes 426000 | tf_op jit(solution)/shard_map/reduce_scatter | solution.py:119
  443.6 1.3 fusion.21
  444.8 0.7 pad_maximum_fusion.3
  445.5 50.5 %all-gather.5.cloned.1.call-done = bf16[256,6656]{1,0:T(8,128)(2,1)} async-done(((bf16[16,6656]{1,0:T(8,128)(2,1)}), bf16[256,6656]{1,0:T(8,128)(2,1)}) %all-gather.5.cloned.1.call-update) | async-done | bytes 3407888 | tf_op jit(solution)/shard_map/all_gather | solution.py:25
  496.1 5.5 %fusion = f32[256,1024]{1,0:T(8,128)S(1)} fusion(bf16[1024,3328]{1,0:T(8,128)(2,1)} %param.12, bf16[256,6656]{1,0:T(8,128)(2,1)} %all-gather.5.cloned.1.call-done), kind=kOutput, calls=%fused_computation.3 | convolution fusion | flops 1744830464 | bytes 9568256 | tf_op jit(solution)/shard_map/dot_general | solution.py:62
  501.6 5.9 %fusion.8 = f32[256,1024]{1,0:T(8,128)} fusion(f32[256,1024]{1,0:T(8,128)S(1)} %fusion, bf16[1024,3328]{1,0:T(8,128)(2,1)} %param.11, bf16[256,6656]{1,0:T(8,128)(2,1)S(1)} %copy-done.7), kind=kOutput, calls=%fused_computation.11 | convolution fusion | flops 1745092608 | bytes 10616832 | tf_op jit(solution)/shard_map/dot_general | solution.py:62
  507.5 4.4 all-to-all-start.1
  512.0 16.2 %all-to-all-done.1 = f32[8,32,1024]{2,1,0:T(8,128)S(1)} async-done(((f32[8,32,1024]{2,1,0:T(8,128)}), f32[8,32,1024]{2,1,0:T(8,128)S(1)}, u32[]{:S(2)}, u32[]{:S(2)}) %all-to-all-start.1) | async-done | bytes 1048608 | tf_op jit(solution)/shard_map/all_to_all | solution.py:39
  528.2 0.7 dynamic-slice_add_fusion
  (41 shorter events, 0.4 us)
Async XLA Ops:
  6.5 229.7 %copy-start = (f32[128256]{0:T(1024)S(1)}, f32[128256]{0:T(1024)}, u32[]{:S(2)}) copy-start(f32[128256]{0:T(1024)} %param.10) | copy-start | bytes 1539076
  8.3 21.0 %all-to-all-start = ((bf16[8,32,1024]{2,1,0:T(8,128)(2,1)}), bf16[8,32,1024]{2,1,0:T(8,128)(2,1)S(1)}, u32[]{:S(2)}, u32[]{:S(2)}) async-start(bf16[8,32,1024]{2,1,0:T(8,128)(2,1)} %broadcast_in_dim.16), calls=%async_computation | async-start | bytes 1048576 | tf_op jit(solution)/shard_map/all_to_all | solution.py:9
  14.6 156.5 %reduce-scatter.3.cloned.1.call-start = ((), (), s32[]{:S(2)}) async-start(), calls=%async_computation.4 | async-start | bytes 14483456 | tf_op jit(solution)/shard_map/reduce_scatter | solution.py:101
  29.3 5.0 slice-start.2
  29.3 5.0 slice-start.3
  34.3 2.0 copy-start.1
  34.3 3.0 copy-start.2
  42.5 180.9 %all-gather.3.cloned.1.call-start = ((), (), s32[]{:S(2)}) async-start(), calls=%async_computation.5 | async-start | bytes 3620864 | tf_op jit(solution)/shard_map/all_gather | solution.py:25
  173.2 166.6 %all-reduce.3.cloned.1.call-start = ((), (), s32[]{:S(2)}) async-start(), calls=%async_computation.8 | async-start | bytes 4194304 | tf_op jit(solution)/shard_map/psum | solution.py:114
  223.4 6.5 %copy-start.6 = (bf16[256,6656]{1,0:T(8,128)(2,1)S(1)}, bf16[256,6656]{1,0:T(8,128)(2,1)}, u32[]{:S(2)}) copy-start(bf16[256,6656]{1,0:T(8,128)(2,1)} %all-gather.3.cloned.1.call-done) | copy-start | bytes 10223620
  229.9 6.3 %copy-start.5 = (s32[256]{0:T(256)S(1)}, s32[256]{0:T(256)}, u32[]{:S(2)}) copy-start(s32[256]{0:T(256)} %param.9) | copy-start | bytes 3076
  235.9 207.6 %reduce-scatter.5.cloned.1.call-start = ((), (), s32[]{:S(2)}) async-start(), calls=%async_computation.6 | async-start | bytes 7241728 | tf_op jit(solution)/shard_map/reduce_scatter | solution.py:119
  339.8 6.8 %slice-start = ((s8[6815744]{0:T(1024)(128)(4,1)}), s8[4194304]{0:T(1024)(128)(4,1)S(1)}, s32[]{:S(2)}) async-start(s8[6815744]{0:T(1024)(128)(4,1)} %bitcast.17), calls=%async_computation.9 | async-start | bytes 8388608
  339.8 6.8 %copy-start.4 = (f32[256,1024]{1,0:T(8,128)S(1)}, f32[256,1024]{1,0:T(8,128)}, u32[]{:S(2)}) copy-start(f32[256,1024]{1,0:T(8,128)} %get-tuple-element.6) | copy-start | bytes 3145732
  341.4 5.2 slice-start.1
  352.3 91.2 %copy-start.3 = (f32[16,13312]{1,0:T(8,128)S(1)}, f32[16,13312]{1,0:T(8,128)}, u32[]{:S(2)}) copy-start(f32[16,13312]{1,0:T(8,128)} %reduce-scatter.3.cloned.1.call-done) | copy-start | bytes 2555908
  352.3 143.7 %all-gather.5.cloned.1.call-start = ((), (), s32[]{:S(2)}) async-start(), calls=%async_computation.7 | async-start | bytes 3620864 | tf_op jit(solution)/shard_map/all_gather | solution.py:25
  496.1 5.6 %copy-start.7 = (bf16[256,6656]{1,0:T(8,128)(2,1)S(1)}, bf16[256,6656]{1,0:T(8,128)(2,1)}, u32[]{:S(2)}) copy-start(bf16[256,6656]{1,0:T(8,128)(2,1)} %all-gather.5.cloned.1.call-done) | copy-start | bytes 10223620
  507.5 20.6 %all-to-all-start.1 = ((f32[8,32,1024]{2,1,0:T(8,128)}), f32[8,32,1024]{2,1,0:T(8,128)S(1)}, u32[]{:S(2)}, u32[]{:S(2)}) async-start(f32[8,32,1024]{2,1,0:T(8,128)} %bitcast.23), calls=%async_computation.3 | async-start | bytes 2097152 | tf_op jit(solution)/shard_map/all_to_all | solution.py:39
Sparse Core Ops, SparseCore 0:
  42.6 128.4 reduce-scatter.2
  173.6 49.7 all-gather.2
  236.1 103.6 all-reduce.2
  352.5 91.0 reduce-scatter.4
  445.9 50.1 all-gather.4
where the time goes:
time: 536 us; the launch traced here: 535 us
  waiting for transfers between devices  439 us (82%)
  matrix products  51.5 us (10%)
  other arithmetic  15.1 us (3%)
  between operations  13.4 us (2%)
  starting transfers between devices  11.2 us (2%)
  local copies, waits for them, and re-layouts  5.77 us (1%)
    reduce_scatter x1, waiting for transfers between devices, on_device(): lax.psum_scatter(jnp.concatenate(project_in(gathered, probe, gate_weight,...  129 us
    psum x1, waiting for transfers between devices, on_device(): output, out_tan = lax.psum((out_pieces[0], out_pieces[1]), 'row')  102 us
    all_gather x2, waiting for transfers between devices, side_by_side(): lax.all_gather(both, axis, axis=dim, tiled=True)  101 us
    reduce_scatter x1, waiting for transfers between devices, on_device(): lax.psum_scatter(jnp.concatenate(paired(cotangent, cot_half, down_weight,...  91.2 us
    dot_general x6, matrix products, matmul(): return jnp.dot(left_rows, weight, preferred_element_type=jnp.float32)  32.8 us
    dot_general x4, matrix products, matmul_trans(): lax.dot_general(left_rows, weight, (((1,), (1,)), ((), ())), preferred_el...  18.7 us
    all_to_all x1, waiting for transfers between devices, summed_on_arrival(): lax.all_to_all(pieces, axis, split_axis=0, concat_axis=0, tiled=True)  16.2 us
  transfers between devices with their start and end apart: 7, of which 6 were waited for; matrix products, arithmetic and copies ran while one was open for 3% of the time, Pallas kernels for 0%

commit v1 on v0

v1 whole, which is shorter than its diff:
```python
import jax
import jax.numpy as jnp
from jax import lax
from jax.sharding import PartitionSpec as P

BF16 = jnp.bfloat16
F16 = jnp.float16
F32 = jnp.float32

SWAP_CORE = [(c, c ^ 1) for c in range(16)]
SWAP_HI = [(c, c ^ 2) for c in range(16)]
SWAP_LO = [(r, r ^ 1) for r in range(8)]


def shift_y(x, d):
    return lax.ppermute(x, "col", [(c, (c + 4 * d) % 16) for c in range(16)])


def shift_z(x, d):
    return lax.ppermute(x, "row", [(r, (r + 2 * d) % 8) for r in range(8)])


def swap_core(x):
    return lax.ppermute(x, "col", SWAP_CORE)


def swap_hi(x):
    return lax.ppermute(x, "col", SWAP_HI)


def swap_lo(x):
    return lax.ppermute(x, "row", SWAP_LO)


def pick(x, i, axis=0):
    return lax.dynamic_index_in_dim(x, i, axis, keepdims=False)


def scatter_sum(x, shift, place, narrow):
    total = pick(x, place(0)).astype(F32)
    arrived = [shift(pick(x, place(d)).astype(narrow), d) for d in (1, 3, 2)]
    for a in arrived:
        total = total + a.astype(F32)
    return total


def gather_ring(x, shift):
    got = {d: shift(x, d) for d in (1, 3, 2)}
    return jnp.stack([x, got[3], got[2], got[1]])


def unpack_signs(packed):
    shifts = jnp.arange(32, dtype=jnp.int32)
    bit_vals = jnp.bitwise_and(jnp.right_shift(packed[:, :, None], shifts), 1)
    return (2 * bit_vals - 1).reshape(packed.shape[0], -1).astype(BF16)


def silu_parts(pre_act):
    sigmoid_pre = jax.nn.sigmoid(pre_act)
    active = pre_act * sigmoid_pre
    slopes = sigmoid_pre * (1.0 + pre_act * (1.0 - sigmoid_pre))
    curves = sigmoid_pre * (1.0 - sigmoid_pre) * (2.0 + pre_act * (1.0 - 2.0 * sigmoid_pre))
    return (active, slopes, curves)


def matmul(left, weight):
    return jnp.dot(left, weight, preferred_element_type=F32)


def matmul_trans(left, weight):
    return lax.dot_general(left, weight, (((1,), (1,)), ((), ())), preferred_element_type=F32)


def on_device(tokens, probe_words, token_ids, loss_weight, gate_weight, up_weight, down_weight):
    col, row = lax.axis_index("col"), lax.axis_index("row")
    core, hi, y = col % 2, (col // 2) % 2, col // 4
    lo, z = row % 2, row // 2
    width = gate_weight.shape[1]
    feats = tokens.shape[1]

    pair = jnp.stack([tokens, swap_lo(tokens)])
    pair = jnp.where(lo == 0, pair, pair[::-1])
    ring = gather_ring(pair, shift_z)
    ring = lax.dynamic_slice_in_dim(jnp.concatenate([ring, ring]), (4 - z) % 4, 4)
    words = probe_words.reshape(4, 2, 32, -1)

    def rows_for(k):
        tok = pick(ring, k, 1).reshape(128, feats)
        signs = unpack_signs(pick(words, k, 1).reshape(128, -1))
        return jnp.concatenate([tok, signs])

    theirs, mine = rows_for(1 - core), rows_for(core)

    def reduced_in(weight):
        arrived = swap_core(matmul(theirs, weight).astype(F16))
        both = (matmul(mine, weight) + arrived.astype(F32)).astype(F16)
        both = jnp.moveaxis(both.reshape(2, 4, 32, width), 1, 0)
        share = scatter_sum(both, shift_y, lambda d: (y + d) % 4, F16)
        share = share.reshape(2, 2, 16, width)
        other = swap_hi(pick(share, 1 - hi, 1).astype(F16))
        return pick(share, hi, 1) + other.astype(F32)

    gate_pre, gate_tan = reduced_in(gate_weight)
    up_pre, up_tan = reduced_in(up_weight)
    active, slopes, curves = silu_parts(gate_pre)
    hidden = (active * up_pre).astype(BF16)
    hidden_tan = (slopes * gate_tan * up_pre + active * up_tan).astype(BF16)

    def gathered_hidden(first, second):
        own = jnp.stack([first, second])
        own = jnp.stack([own, swap_hi(own)])
        own = gather_ring(own, shift_y)
        return jnp.stack([own, swap_core(own)], axis=1)

    def reduced_out(partial):
        share = scatter_sum(partial, shift_z, lambda d: (z + d - y) % 4, BF16)
        mine_at = (lo - core) % 2
        other = swap_lo(pick(share, 1 - mine_at).astype(BF16))
        total = pick(share, mine_at) + other.astype(F32)
        total = jnp.where(hi == 0, total, total[::-1])
        return jnp.moveaxis(total, 0, 1).reshape(-1, 32, feats)

    both = gathered_hidden(hidden, hidden_tan).reshape(512, width)
    output, out_tan = reduced_out(matmul(both, down_weight).reshape(4, 2, 2, 2, 16, feats))

    own_ids = lax.dynamic_slice_in_dim(token_ids, row * 32, 32)
    weight_tok = jnp.take(loss_weight, own_ids)[:, None]
    own_probe = unpack_signs(lax.dynamic_slice_in_dim(probe_words, row * 32, 32)).astype(F32)
    cotangent = (weight_tok * (tokens.astype(F32) + output)).astype(BF16)
    cot_tan = weight_tok * (own_probe + out_tan)

    own = jnp.stack([cotangent, cot_tan.astype(BF16)])
    own = jnp.stack([own, swap_lo(own)])
    cots = gather_ring(own, shift_z)
    theirs_at = (1 - core - lo) % 2
    cots_theirs = pick(cots, theirs_at, 1).reshape(256, feats)
    cots_mine = pick(cots, 1 - theirs_at, 1).reshape(256, feats)
    arrived = swap_core(matmul_trans(cots_theirs, down_weight).astype(BF16))
    back = matmul_trans(cots_mine, down_weight) + arrived.astype(F32)
    share = scatter_sum(back.reshape(4, 2, 32, width), shift_y, lambda d: (y + d - z) % 4, BF16)
    share = share.reshape(2, 2, 16, width)
    other = swap_hi(pick(share, 1 - hi, 1).astype(BF16))
    backward, back_tan = pick(share, hi, 1) + other.astype(F32)

    gate_back = (
        back_tan * up_pre * slopes
        + backward * up_tan * slopes
        + backward * up_pre * curves * gate_tan
    ).astype(BF16)
    up_back = (back_tan * active + backward * slopes * gate_tan).astype(BF16)
    both = gathered_hidden(gate_back, up_back)
    gates = both[:, :, :, 0].reshape(256, width)
    ups = both[:, :, :, 1].reshape(256, width)
    partial = matmul_trans(gates, gate_weight) + matmul_trans(ups, up_weight)
    summed = reduced_out(partial.reshape(4, 2, 2, 1, 16, feats))
    return cot_tan + summed[0]


def solution(mesh):
    return jax.shard_map(
        on_device,
        mesh=mesh,
        in_specs=(
            P("row", "col"),
            P(None, "col"),
            P(),
            P(),
            P("col", "row"),
            P("col", "row"),
            P("row", "col"),
        ),
        out_specs=P("row", "col"),
        check_vma=False,
    )
```

time: 536 us -> 279 us (0.52)
  waiting for transfers between devices: 439 us -> 153 us
  starting transfers between devices: 11.2 us -> 59.7 us
  between operations: 13.4 us -> 0.62 us
  matrix products: 51.5 us -> 41.9 us
  local copies, waits for them, and re-layouts: 5.77 us -> 12.9 us
    reduce_scatter x2 -> x0, waiting for transfers between devices: 220 us -> none  [the longest x1 129 us: on_device(): lax.psum_scatter(jnp.concatenate(project_in(gathered, probe, gate_weight,...]
    ppermute x0 -> x41, waiting for transfers between devices: none -> 153 us  [the longest x15 72.1 us: shift_y(): return lax.ppermute(x, 'col', [(c, (c + 4 * d) % 16) for c in range(16)])]
    psum x1 -> x0, waiting for transfers between devices: 102 us -> none  [on_device(): output, out_tan = lax.psum((out_pieces[0], out_pieces[1]), 'row')]
    all_gather x2 -> x0, waiting for transfers between devices: 101 us -> none  [side_by_side(): lax.all_gather(both, axis, axis=dim, tiled=True)]
    ppermute x0 -> x41, starting transfers between devices: none -> 59.7 us  [the longest x15 26.2 us: shift_y(): return lax.ppermute(x, 'col', [(c, (c + 4 * d) % 16) for c in range(16)])]
    all_to_all x2 -> x0, waiting for transfers between devices: 16.2 us -> none  [the longest x1 16.2 us: summed_on_arrival(): lax.all_to_all(pieces, axis, split_axis=0, concat_axis=0, tiled=True)]
    all_to_all x2 -> x0, starting transfers between devices: 10.8 us -> none  [the longest x1 6.35 us: copy_for_each(): return lax.all_to_all(copies, axis, split_axis=0, concat_axis=0, tiled=True)]
    concatenate x4 -> x0, other arithmetic: 10.1 us -> none  [the longest x1 5.13 us: on_device(): jnp.concatenate(project_in(gathered, probe, gate_weight, up_weight), axis=1)]
  transfers between devices with their start and end apart: 7 -> 41, of which waited for: 6 -> 33; matrix products, arithmetic and copies ran while one was open for 3% -> 7% of each run, Pallas kernels for 0% -> 0%
where the time goes in v1:
time: 279 us; the launch traced here: 278 us
  waiting for transfers between devices  153 us (55%)
  starting transfers between devices  59.7 us (21%)
  matrix products  41.9 us (15%)
  local copies, waits for them, and re-layouts  12.9 us (5%)
  other arithmetic  10.1 us (4%)
    ppermute x15, waiting for transfers between devices, shift_y(): return lax.ppermute(x, 'col', [(c, (c + 4 * d) % 16) for c in range(16)])  72.1 us
    ppermute x12, waiting for transfers between devices, shift_z(): return lax.ppermute(x, 'row', [(r, (r + 2 * d) % 8) for r in range(8)])  34.1 us
    dot_general x5, matrix products, matmul(): return jnp.dot(left, weight, preferred_element_type=F32)  26.5 us
    ppermute x15, starting transfers between devices, shift_y(): return lax.ppermute(x, 'col', [(c, (c + 4 * d) % 16) for c in range(16)])  26.2 us
    ppermute x5, waiting for transfers between devices, swap_hi(): return lax.ppermute(x, 'col', SWAP_HI)  23.4 us
    ppermute x12, starting transfers between devices, shift_z(): return lax.ppermute(x, 'row', [(r, (r + 2 * d) % 8) for r in range(8)])  16.1 us
    dot_general x4, matrix products, matmul_trans(): lax.dot_general(left, weight, (((1,), (1,)), ((), ())), preferred_element...  15.4 us
    ppermute x4, waiting for transfers between devices, swap_lo(): return lax.ppermute(x, 'row', SWAP_LO)  12 us
  transfers between devices with their start and end apart: 41, of which 33 were waited for; matrix products, arithmetic and copies ran while one was open for 7% of the time, Pallas kernels for 0%

profile of v1, /device:TPU:0, one launch (start us, length us, event | category | flops | bytes accessed | tf_op | source)
XLA Modules:
  0.0 278.5 jit_solution(7157200359639723237)
XLA Ops:
  4.5 4.2 %collective-permute-start.1 = (bf16[2,32,1024]{2,1,0:T(8,128)(2,1)S(1)}, bf16[2,32,1024]{2,1,0:T(8,128)(2,1)S(1)}, u32[]{:S(2)}, u32[]{:S(2)}) collective-permute-start(bf16[2,32,1024]{2,1,0:T(8,128)(2,1)S(1)} %get-tuple-element.6), channel_id=1, source_target_pairs={{0,96},{16,112},{32,0},{48,16},{64,32},{80,48},{96,64},{112,80},{1... | collective-permute-start | bytes 393224 | tf_op jit(solution)/shard_map/ppermute | solution.py:20
  11.9 4.8 %collective-permute-done.2 = bf16[2,32,1024]{2,1,0:T(8,128)(2,1)S(1)} collective-permute-done((bf16[2,32,1024]{2,1,0:T(8,128)(2,1)S(1)}, bf16[2,32,1024]{2,1,0:T(8,128)(2,1)S(1)}, u32[]{:S(2)}, u32[]{:S(2)}) %collective-permute-start.2) | collective-permute-done | bytes 131104 | tf_op jit(solution)/shard_map/ppermute | solution.py:20
  17.8 6.3 %convolution_convert_fusion.2 = f16[256,3328]{1,0:T(8,128)(2,1)} fusion(bf16[1024,3328]{1,0:T(8,128)(2,1)} %param.11, bf16[128,1024]{1,0:T(8,128)(2,1)S(1)} %copy-done.8, bf16[128,1024]{1,0:T(8,128)(2,1)S(1)} %bitcast.237), kind=kOutput, calls=%fused_computation.5 | convolution fusion | flops 1746731008 | bytes 9043968 | tf_op jit(solution)/shard_map/dot_general | solution.py:67
  24.1 3.2 %convolution_convert_fusion.1 = f16[256,3328]{1,0:T(8,128)(2,1)} fusion(bf16[1024,3328]{1,0:T(8,128)(2,1)S(1)} %bitcast.251, bf16[128,1024]{1,0:T(8,128)(2,1)S(1)} %copy-done.8, bf16[128,1024]{1,0:T(8,128)(2,1)S(1)} %bitcast.238), kind=kOutput, calls=%fused_computation.4 | convolution fusion | flops 1746731008 | bytes 9043968 | tf_op jit(solution)/shard_map/dot_general | solution.py:67
  28.0 5.3 %add_convert_fusion.1 = f16[256,3328]{1,0:T(8,128)(2,1)S(1)} fusion(f16[256,3328]{1,0:T(8,128)(2,1)} %collective-permute-done.4, bf16[1024,3328]{1,0:T(8,128)(2,1)} %param.11, bf16[128,1024]{1,0:T(8,128)(2,1)S(1)} %copy-done.6, bf16[128,1024]{1,0:T(8,128)(2,1)S(1)} %bitcast.235), kind=kOutput, calls=%fused_computation.13 | convolution fusion | flops 1748434944 | bytes 10747904 | tf_op jit(solution)/shard_map/dot_general | solution.py:67
  38.9 5.3 %add_convert_fusion = f16[256,3328]{1,0:T(8,128)(2,1)S(1)} fusion(f16[256,3328]{1,0:T(8,128)(2,1)} %collective-permute-done.9, bf16[1024,3328]{1,0:T(8,128)(2,1)} %param.12, bf16[128,1024]{1,0:T(8,128)(2,1)S(1)} %copy-done.7, bf16[128,1024]{1,0:T(8,128)(2,1)S(1)} %bitcast.236), kind=kOutput, calls=%fused_computation.12 | convolution fusion | flops 1748434944 | bytes 10747904 | tf_op jit(solution)/shard_map/dot_general | solution.py:67
  50.5 7.3 %collective-permute-start.12 = (f16[2,32,3328]{2,1,0:T(8,128)(2,1)S(1)}, f16[2,32,3328]{2,1,0:T(8,128)(2,1)}, u32[]{:S(2)}, u32[]{:S(2)}) collective-permute-start(f16[2,32,3328]{2,1,0:T(8,128)(2,1)S(1)} %get-tuple-element.23), channel_id=1, source_target_pairs={{0,8},{1,9},{2,10},{3,11},{4,12},{5,13},{6,14},{7,15},{8,0},{9,1},... | collective-permute-start | bytes 1277960 | tf_op jit(solution)/shard_map/ppermute | solution.py:16
  58.1 9.0 %collective-permute-done.10 = f16[2,32,3328]{2,1,0:T(8,128)(2,1)} collective-permute-done((f16[2,32,3328]{2,1,0:T(8,128)(2,1)}, f16[2,32,3328]{2,1,0:T(8,128)(2,1)}, u32[]{:S(2)}, u32[]{:S(2)}) %collective-permute-start.10) | collective-permute-done | bytes 426016 | tf_op jit(solution)/shard_map/ppermute | solution.py:16
  67.1 6.5 %collective-permute-done.11 = f16[2,32,3328]{2,1,0:T(8,128)(2,1)} collective-permute-done((f16[2,32,3328]{2,1,0:T(8,128)(2,1)}, f16[2,32,3328]{2,1,0:T(8,128)(2,1)}, u32[]{:S(2)}, u32[]{:S(2)}) %collective-permute-start.11) | collective-permute-done | bytes 426016 | tf_op jit(solution)/shard_map/ppermute | solution.py:16
  77.8 3.1 %collective-permute-start.8 = (f16[2,16,3328]{2,1,0:T(8,128)(2,1)S(1)}, f16[2,16,3328]{2,1,0:T(8,128)(2,1)S(1)}, u32[]{:S(2)}, u32[]{:S(2)}) collective-permute-start(f16[2,16,3328]{2,1,0:T(8,128)(2,1)S(1)} %fusion.32), channel_id=1, source_target_pairs={{0,2},{1,3},{2,0},{3,1},{4,6},{5,7},{6,4},{7,5},{8,10},{9,11},{10,... | collective-permute-start | bytes 638984 | tf_op jit(solution)/shard_map/ppermute | solution.py:28
  81.5 6.0 %collective-permute-done.8 = f16[2,16,3328]{2,1,0:T(8,128)(2,1)S(1)} collective-permute-done((f16[2,16,3328]{2,1,0:T(8,128)(2,1)S(1)}, f16[2,16,3328]{2,1,0:T(8,128)(2,1)S(1)}, u32[]{:S(2)}, u32[]{:S(2)}) %collective-permute-start.8) | collective-permute-done | bytes 213024 | tf_op jit(solution)/shard_map/ppermute | solution.py:28
  93.7 4.3 %collective-permute-done.14 = bf16[2,16,3328]{2,1,0:T(8,128)(2,1)S(1)} collective-permute-done((bf16[2,16,3328]{2,1,0:T(8,128)(2,1)S(1)}, bf16[2,16,3328]{2,1,0:T(8,128)(2,1)S(1)}, u32[]{:S(2)}, u32[]{:S(2)}) %collective-permute-start.14) | collective-permute-done | bytes 213024 | tf_op jit(solution)/shard_map/ppermute | solution.py:28
  101.1 9.8 %collective-permute-done.15 = bf16[2,2,16,3328]{3,2,1,0:T(8,128)(2,1)S(1)} collective-permute-done((bf16[2,2,16,3328]{3,2,1,0:T(8,128)(2,1)S(1)}, bf16[2,2,16,3328]{3,2,1,0:T(8,128)(2,1)S(1)}, u32[]{:S(2)}, u32[]{:S(2)}) %collective-permute-start.15) | collective-permute-done | bytes 426016 | tf_op jit(solution)/shard_map/ppermute | solution.py:16
  113.7 5.1 %collective-permute-done.17 = bf16[2,2,16,3328]{3,2,1,0:T(8,128)(2,1)S(1)} collective-permute-done((bf16[2,2,16,3328]{3,2,1,0:T(8,128)(2,1)S(1)}, bf16[2,2,16,3328]{3,2,1,0:T(8,128)(2,1)S(1)}, u32[]{:S(2)}, u32[]{:S(2)}) %collective-permute-start.17) | collective-permute-done | bytes 426016 | tf_op jit(solution)/shard_map/ppermute | solution.py:16
  120.3 3.9 %collective-permute-done.18 = bf16[4,2,2,16,3328]{4,3,2,1,0:T(8,128)(2,1)} collective-permute-done((bf16[4,2,2,16,3328]{4,3,2,1,0:T(8,128)(2,1)}, bf16[4,2,2,16,3328]{4,3,2,1,0:T(8,128)(2,1)}, u32[]{:S(2)}, u32[]{:S(2)}) %collective-permute-start.18) | collective-permute-done | bytes 1703968 | tf_op jit(solution)/shard_map/ppermute | solution.py:24
  124.2 6.4 %fusion = f32[4,2,2,2,16,1024]{5,4,3,2,1,0:T(8,128)S(1)} fusion(bf16[3328,1024]{1,0:T(8,128)(2,1)} %param.13, bf16[4,1,2,2,16,3328]{5,4,3,2,1,0:T(8,128)(2,1)} %bitcast.40, bf16[4,1,2,2,16,3328]{5,4,3,2,1,0:T(8,128)(2,1)S(1)} %get-tuple-element.17), kind=kOutput, calls=%fused_computation.1 | convolution fusion | flops 3491364864 | bytes 12320768 | tf_op jit(solution)/shard_map/dot_general | solution.py:67
  132.1 3.2 %collective-permute-start.20 = (bf16[2,2,2,16,1024]{4,3,2,1,0:T(8,128)(2,1)S(1)}, bf16[2,2,2,16,1024]{4,3,2,1,0:T(8,128)(2,1)S(1)}, u32[]{:S(2)}, u32[]{:S(2)}) collective-permute-start(bf16[2,2,2,16,1024]{4,3,2,1,0:T(8,128)(2,1)S(1)} %get-tuple-element.14), channel_id=1, source_target_pairs={{0,96},{16,112},{32,0},{48,16},{64,32},{80,48},{96,64},{112,80},{1... | collective-permute-start | bytes 786440 | tf_op jit(solution)/shard_map/ppermute | solution.py:20
  136.8 10.5 %collective-permute-done.19 = bf16[2,2,2,16,1024]{4,3,2,1,0:T(8,128)(2,1)S(1)} collective-permute-done((bf16[2,2,2,16,1024]{4,3,2,1,0:T(8,128)(2,1)S(1)}, bf16[2,2,2,16,1024]{4,3,2,1,0:T(8,128)(2,1)S(1)}, u32[]{:S(2)}, u32[]{:S(2)}) %collective-permute-start.19) | collective-permute-done | bytes 262176 | tf_op jit(solution)/shard_map/ppermute | solution.py:20
  149.7 3.9 %collective-permute-done.22 = bf16[2,2,16,1024]{3,2,1,0:T(8,128)(2,1)S(1)} collective-permute-done((bf16[2,2,16,1024]{3,2,1,0:T(8,128)(2,1)S(1)}, bf16[2,2,16,1024]{3,2,1,0:T(8,128)(2,1)S(1)}, u32[]{:S(2)}, u32[]{:S(2)}) %collective-permute-start.22) | collective-permute-done | bytes 131104 | tf_op jit(solution)/shard_map/ppermute | solution.py:32
  155.0 4.0 %collective-permute-done.23 = bf16[2,32,1024]{2,1,0:T(8,128)(2,1)S(1)} collective-permute-done((bf16[2,32,1024]{2,1,0:T(8,128)(2,1)S(1)}, bf16[2,32,1024]{2,1,0:T(8,128)(2,1)S(1)}, u32[]{:S(2)}, u32[]{:S(2)}) %collective-permute-start.23) | collective-permute-done | bytes 131104 | tf_op jit(solution)/shard_map/ppermute | solution.py:32
  163.0 7.1 %collective-permute-done.24 = bf16[2,2,32,1024]{3,2,1,0:T(8,128)(2,1)S(1)} collective-permute-done((bf16[2,2,32,1024]{3,2,1,0:T(8,128)(2,1)S(1)}, bf16[2,2,32,1024]{3,2,1,0:T(8,128)(2,1)S(1)}, u32[]{:S(2)}, u32[]{:S(2)}) %collective-permute-start.24) | collective-permute-done | bytes 262176 | tf_op jit(solution)/shard_map/ppermute | solution.py:20
  173.8 6.1 %convolution_convert_fusion = bf16[256,3328]{1,0:T(8,128)(2,1)} fusion(bf16[256,1024]{1,0:T(8,128)(2,1)S(1)} %bitcast.225, bf16[3328,1024]{1,0:T(8,128)(2,1)} %param.13), kind=kOutput, calls=%fused_computation.3 | convolution fusion | flops 1745682432 | bytes 9043968 | tf_op jit(solution)/shard_map/dot_general | solution.py:71
  179.9 3.9 %collective-permute-done.27 = bf16[256,3328]{1,0:T(8,128)(2,1)} collective-permute-done((bf16[256,3328]{1,0:T(8,128)(2,1)}, bf16[256,3328]{1,0:T(8,128)(2,1)}, u32[]{:S(2)}, u32[]{:S(2)}) %collective-permute-start.27) | collective-permute-done | bytes 1703968 | tf_op jit(solution)/shard_map/ppermute | solution.py:24
  183.8 5.4 %convert_add_fusion = f32[256,3328]{1,0:T(8,128)S(1)} fusion(bf16[256,3328]{1,0:T(8,128)(2,1)} %collective-permute-done.27, bf16[256,1024]{1,0:T(8,128)(2,1)S(1)} %bitcast.224, bf16[3328,1024]{1,0:T(8,128)(2,1)} %param.13), kind=kOutput, calls=%fused_computation.11 | convolution fusion | flops 1746534400 | bytes 12451840 | tf_op jit(solution)/shard_map/dot_general | solution.py:71
  195.7 18.7 %collective-permute-done.28 = bf16[2,32,3328]{2,1,0:T(8,128)(2,1)S(1)} collective-permute-done((bf16[2,32,3328]{2,1,0:T(8,128)(2,1)}, bf16[2,32,3328]{2,1,0:T(8,128)(2,1)S(1)}, u32[]{:S(2)}, u32[]{:S(2)}) %collective-permute-start.28) | collective-permute-done | bytes 426016 | tf_op jit(solution)/shard_map/ppermute | solution.py:16
  218.4 5.4 %collective-permute-done.31 = bf16[2,16,3328]{2,1,0:T(8,128)(2,1)S(1)} collective-permute-done((bf16[2,16,3328]{2,1,0:T(8,128)(2,1)S(1)}, bf16[2,16,3328]{2,1,0:T(8,128)(2,1)S(1)}, u32[]{:S(2)}, u32[]{:S(2)}) %collective-permute-start.31) | collective-permute-done | bytes 213024 | tf_op jit(solution)/shard_map/ppermute | solution.py:28
  226.8 4.8 %collective-permute-done.32 = bf16[2,16,3328]{2,1,0:T(8,128)(2,1)S(1)} collective-permute-done((bf16[2,16,3328]{2,1,0:T(8,128)(2,1)S(1)}, bf16[2,16,3328]{2,1,0:T(8,128)(2,1)S(1)}, u32[]{:S(2)}, u32[]{:S(2)}) %collective-permute-start.32) | collective-permute-done | bytes 213024 | tf_op jit(solution)/shard_map/ppermute | solution.py:28
  235.4 14.4 %collective-permute-done.33 = bf16[2,2,16,3328]{3,2,1,0:T(8,128)(2,1)S(1)} collective-permute-done((bf16[2,2,16,3328]{3,2,1,0:T(8,128)(2,1)S(1)}, bf16[2,2,16,3328]{3,2,1,0:T(8,128)(2,1)S(1)}, u32[]{:S(2)}, u32[]{:S(2)}) %collective-permute-start.33) | collective-permute-done | bytes 426016 | tf_op jit(solution)/shard_map/ppermute | solution.py:16
  249.8 3.6 %collective-permute-done.35 = bf16[2,2,16,3328]{3,2,1,0:T(8,128)(2,1)S(1)} collective-permute-done((bf16[2,2,16,3328]{3,2,1,0:T(8,128)(2,1)S(1)}, bf16[2,2,16,3328]{3,2,1,0:T(8,128)(2,1)S(1)}, u32[]{:S(2)}, u32[]{:S(2)}) %collective-permute-start.35) | collective-permute-done | bytes 426016 | tf_op jit(solution)/shard_map/ppermute | solution.py:16
  253.8 3.6 %collective-permute-done.36 = bf16[4,2,2,16,3328]{4,3,2,1,0:T(8,128)(2,1)S(1)} collective-permute-done((bf16[4,2,2,16,3328]{4,3,2,1,0:T(8,128)(2,1)S(1)}, bf16[4,2,2,16,3328]{4,3,2,1,0:T(8,128)(2,1)S(1)}, u32[]{:S(2)}, u32[]{:S(2)}) %collective-permute-start.36) | collective-permute-done | bytes 1703968 | tf_op jit(solution)/shard_map/ppermute | solution.py:24
  263.4 3.2 %collective-permute-start.38 = (bf16[2,2,1,16,1024]{4,3,1,0,2:T(8,128)(2,1)S(1)}, bf16[2,2,1,16,1024]{4,3,1,0,2:T(8,128)(2,1)S(1)}, u32[]{:S(2)}, u32[]{:S(2)}) collective-permute-start(bf16[2,2,1,16,1024]{4,3,1,0,2:T(8,128)(2,1)S(1)} %get-tuple-element.26), channel_id=1, source_target_pairs={{0,96},{16,112},{32,0},{48,16},{64,32},{80,48},{96,64},{112,80},{1... | collective-permute-start | bytes 393224 | tf_op jit(solution)/shard_map/ppermute | solution.py:20
  266.8 3.4 %collective-permute-done.37 = bf16[2,2,1,16,1024]{4,3,1,0,2:T(8,128)(2,1)S(1)} collective-permute-done((bf16[2,2,1,16,1024]{4,3,1,0,2:T(8,128)(2,1)S(1)}, bf16[2,2,1,16,1024]{4,3,1,0,2:T(8,128)(2,1)S(1)}, u32[]{:S(2)}, u32[]{:S(2)}) %collective-permute-start.37) | collective-permute-done | bytes 131104 | tf_op jit(solution)/shard_map/ppermute | solution.py:20
  (171 shorter events, 85.8 us)
Async XLA Ops:
  4.5 7.3 %collective-permute-start.1 = (bf16[2,32,1024]{2,1,0:T(8,128)(2,1)S(1)}, bf16[2,32,1024]{2,1,0:T(8,128)(2,1)S(1)}, u32[]{:S(2)}, u32[]{:S(2)}) collective-permute-start(bf16[2,32,1024]{2,1,0:T(8,128)(2,1)S(1)} %get-tuple-element.6), channel_id=1, source_target_pairs={{0,96},{16,112},{32,0},{48,16},{64,32},{80,48},{96,64},{112,80},{1... | collective-permute-start | bytes 393224 | tf_op jit(solution)/shard_map/ppermute | solution.py:20
  9.8 6.9 %collective-permute-start.2 = (bf16[2,32,1024]{2,1,0:T(8,128)(2,1)S(1)}, bf16[2,32,1024]{2,1,0:T(8,128)(2,1)S(1)}, u32[]{:S(2)}, u32[]{:S(2)}) collective-permute-start(bf16[2,32,1024]{2,1,0:T(8,128)(2,1)S(1)} %get-tuple-element.6), channel_id=1, source_target_pairs={{0,64},{16,80},{32,96},{48,112},{64,0},{80,16},{96,32},{112,48},{1... | collective-permute-start | bytes 393224 | tf_op jit(solution)/shard_map/ppermute | solution.py:20
  9.8 7.8 %collective-permute-start.3 = (bf16[2,32,1024]{2,1,0:T(8,128)(2,1)S(1)}, bf16[2,32,1024]{2,1,0:T(8,128)(2,1)S(1)}, u32[]{:S(2)}, u32[]{:S(2)}) collective-permute-start(bf16[2,32,1024]{2,1,0:T(8,128)(2,1)S(1)} %get-tuple-element.6), channel_id=1, source_target_pairs={{0,32},{16,48},{32,64},{48,80},{64,96},{80,112},{96,0},{112,16},{1... | collective-permute-start | bytes 393224 | tf_op jit(solution)/shard_map/ppermute | solution.py:20
  27.3 11.6 %collective-permute-start.9 = (f16[256,3328]{1,0:T(8,128)(2,1)}, f16[256,3328]{1,0:T(8,128)(2,1)}, u32[]{:S(2)}, u32[]{:S(2)}) collective-permute-start(f16[256,3328]{1,0:T(8,128)(2,1)} %convolution_convert_fusion.1), channel_id=1, source_target_pairs={{0,1},{1,0},{2,3},{3,2},{4,5},{5,4},{6,7},{7,6},{8,9},{9,8},{10,11... | collective-permute-start | bytes 5111816 | tf_op jit(solution)/shard_map/ppermute | solution.py:24
  33.6 16.2 %collective-permute-start.5 = (f16[2,32,3328]{2,1,0:T(8,128)(2,1)S(1)}, f16[2,32,3328]{2,1,0:T(8,128)(2,1)S(1)}, u32[]{:S(2)}, u32[]{:S(2)}) collective-permute-start(f16[2,32,3328]{2,1,0:T(8,128)(2,1)S(1)} %get-tuple-element.19), channel_id=1, source_target_pairs={{0,4},{1,5},{2,6},{3,7},{4,8},{5,9},{6,10},{7,11},{8,12},{9,13},{1... | collective-permute-start | bytes 1277960 | tf_op jit(solution)/shard_map/ppermute | solution.py:16
  35.2 22.6 %collective-permute-start.6 = (f16[2,32,3328]{2,1,0:T(8,128)(2,1)S(1)}, f16[2,32,3328]{2,1,0:T(8,128)(2,1)}, u32[]{:S(2)}, u32[]{:S(2)}) collective-permute-start(f16[2,32,3328]{2,1,0:T(8,128)(2,1)S(1)} %get-tuple-element.21), channel_id=1, source_target_pairs={{0,12},{1,13},{2,14},{3,15},{4,0},{5,1},{6,2},{7,3},{8,4},{9,5},{1... | collective-permute-start | bytes 1277960 | tf_op jit(solution)/shard_map/ppermute | solution.py:16
  36.9 21.2 %collective-permute-start.7 = (f16[2,32,3328]{2,1,0:T(8,128)(2,1)S(1)}, f16[2,32,3328]{2,1,0:T(8,128)(2,1)}, u32[]{:S(2)}, u32[]{:S(2)}) collective-permute-start(f16[2,32,3328]{2,1,0:T(8,128)(2,1)S(1)} %get-tuple-element.20), channel_id=1, source_target_pairs={{0,8},{1,9},{2,10},{3,11},{4,12},{5,13},{6,14},{7,15},{8,0},{9,1},... | collective-permute-start | bytes 1277960 | tf_op jit(solution)/shard_map/ppermute | solution.py:16
  46.5 20.6 %collective-permute-start.10 = (f16[2,32,3328]{2,1,0:T(8,128)(2,1)}, f16[2,32,3328]{2,1,0:T(8,128)(2,1)}, u32[]{:S(2)}, u32[]{:S(2)}) collective-permute-start(f16[2,32,3328]{2,1,0:T(8,128)(2,1)} %get-tuple-element.22), channel_id=1, source_target_pairs={{0,4},{1,5},{2,6},{3,7},{4,8},{5,9},{6,10},{7,11},{8,12},{9,13},{1... | collective-permute-start | bytes 1277960 | tf_op jit(solution)/shard_map/ppermute | solution.py:16
  47.2 26.4 %collective-permute-start.11 = (f16[2,32,3328]{2,1,0:T(8,128)(2,1)}, f16[2,32,3328]{2,1,0:T(8,128)(2,1)}, u32[]{:S(2)}, u32[]{:S(2)}) collective-permute-start(f16[2,32,3328]{2,1,0:T(8,128)(2,1)} %get-tuple-element.24), channel_id=1, source_target_pairs={{0,12},{1,13},{2,14},{3,15},{4,0},{5,1},{6,2},{7,3},{8,4},{9,5},{1... | collective-permute-start | bytes 1277960 | tf_op jit(solution)/shard_map/ppermute | solution.py:16
  50.5 24.9 %collective-permute-start.12 = (f16[2,32,3328]{2,1,0:T(8,128)(2,1)S(1)}, f16[2,32,3328]{2,1,0:T(8,128)(2,1)}, u32[]{:S(2)}, u32[]{:S(2)}) collective-permute-start(f16[2,32,3328]{2,1,0:T(8,128)(2,1)S(1)} %get-tuple-element.23), channel_id=1, source_target_pairs={{0,8},{1,9},{2,10},{3,11},{4,12},{5,13},{6,14},{7,15},{8,0},{9,1},... | collective-permute-start | bytes 1277960 | tf_op jit(solution)/shard_map/ppermute | solution.py:16
  77.8 9.7 %collective-permute-start.8 = (f16[2,16,3328]{2,1,0:T(8,128)(2,1)S(1)}, f16[2,16,3328]{2,1,0:T(8,128)(2,1)S(1)}, u32[]{:S(2)}, u32[]{:S(2)}) collective-permute-start(f16[2,16,3328]{2,1,0:T(8,128)(2,1)S(1)} %fusion.32), channel_id=1, source_target_pairs={{0,2},{1,3},{2,0},{3,1},{4,6},{5,7},{6,4},{7,5},{8,10},{9,11},{10,... | collective-permute-start | bytes 638984 | tf_op jit(solution)/shard_map/ppermute | solution.py:28
  80.9 9.5 %collective-permute-start.13 = (f16[2,16,3328]{2,1,0:T(8,128)(2,1)S(1)}, f16[2,16,3328]{2,1,0:T(8,128)(2,1)S(1)}, u32[]{:S(2)}, u32[]{:S(2)}) collective-permute-start(f16[2,16,3328]{2,1,0:T(8,128)(2,1)S(1)} %fusion.33), channel_id=1, source_target_pairs={{0,2},{1,3},{2,0},{3,1},{4,6},{5,7},{6,4},{7,5},{8,10},{9,11},{10,... | collective-permute-start | bytes 638984 | tf_op jit(solution)/shard_map/ppermute | solution.py:28
  90.6 7.4 %collective-permute-start.14 = (bf16[2,16,3328]{2,1,0:T(8,128)(2,1)S(1)}, bf16[2,16,3328]{2,1,0:T(8,128)(2,1)S(1)}, u32[]{:S(2)}, u32[]{:S(2)}) collective-permute-start(bf16[2,16,3328]{2,1,0:T(8,128)(2,1)S(1)} %get-tuple-element.46), channel_id=1, source_target_pairs={{0,2},{1,3},{2,0},{3,1},{4,6},{5,7},{6,4},{7,5},{8,10},{9,11},{10,... | collective-permute-start | bytes 638984 | tf_op jit(solution)/shard_map/ppermute | solution.py:28
  98.1 12.8 %collective-permute-start.15 = (bf16[2,2,16,3328]{3,2,1,0:T(8,128)(2,1)S(1)}, bf16[2,2,16,3328]{3,2,1,0:T(8,128)(2,1)S(1)}, u32[]{:S(2)}, u32[]{:S(2)}) collective-permute-start(bf16[2,2,16,3328]{3,2,1,0:T(8,128)(2,1)S(1)} %get-tuple-element.38), channel_id=1, source_target_pairs={{0,12},{1,13},{2,14},{3,15},{4,0},{5,1},{6,2},{7,3},{8,4},{9,5},{1... | collective-permute-start | bytes 1277960 | tf_op jit(solution)/shard_map/ppermute | solution.py:16
  99.5 14.2 %collective-permute-start.16 = (bf16[2,2,16,3328]{3,2,1,0:T(8,128)(2,1)S(1)}, bf16[2,2,16,3328]{3,2,1,0:T(8,128)(2,1)S(1)}, u32[]{:S(2)}, u32[]{:S(2)}) collective-permute-start(bf16[2,2,16,3328]{3,2,1,0:T(8,128)(2,1)S(1)} %get-tuple-element.38), channel_id=1, source_target_pairs={{0,8},{1,9},{2,10},{3,11},{4,12},{5,13},{6,14},{7,15},{8,0},{9,1},... | collective-permute-start | bytes 1277960 | tf_op jit(solution)/shard_map/ppermute | solution.py:16
  101.1 17.7 %collective-permute-start.17 = (bf16[2,2,16,3328]{3,2,1,0:T(8,128)(2,1)S(1)}, bf16[2,2,16,3328]{3,2,1,0:T(8,128)(2,1)S(1)}, u32[]{:S(2)}, u32[]{:S(2)}) collective-permute-start(bf16[2,2,16,3328]{3,2,1,0:T(8,128)(2,1)S(1)} %get-tuple-element.38), channel_id=1, source_target_pairs={{0,4},{1,5},{2,6},{3,7},{4,8},{5,9},{6,10},{7,11},{8,12},{9,13},{1... | collective-permute-start | bytes 1277960 | tf_op jit(solution)/shard_map/ppermute | solution.py:16
  132.0 15.2 %collective-permute-start.19 = (bf16[2,2,2,16,1024]{4,3,2,1,0:T(8,128)(2,1)S(1)}, bf16[2,2,2,16,1024]{4,3,2,1,0:T(8,128)(2,1)S(1)}, u32[]{:S(2)}, u32[]{:S(2)}) collective-permute-start(bf16[2,2,2,16,1024]{4,3,2,1,0:T(8,128)(2,1)S(1)} %get-tuple-element.12), channel_id=1, source_target_pairs={{0,32},{16,48},{32,64},{48,80},{64,96},{80,112},{96,0},{112,16},{1... | collective-permute-start | bytes 786440 | tf_op jit(solution)/shard_map/ppermute | solution.py:20
  132.1 15.2 %collective-permute-start.20 = (bf16[2,2,2,16,1024]{4,3,2,1,0:T(8,128)(2,1)S(1)}, bf16[2,2,2,16,1024]{4,3,2,1,0:T(8,128)(2,1)S(1)}, u32[]{:S(2)}, u32[]{:S(2)}) collective-permute-start(bf16[2,2,2,16,1024]{4,3,2,1,0:T(8,128)(2,1)S(1)} %get-tuple-element.14), channel_id=1, source_target_pairs={{0,96},{16,112},{32,0},{48,16},{64,32},{80,48},{96,64},{112,80},{1... | collective-permute-start | bytes 786440 | tf_op jit(solution)/shard_map/ppermute | solution.py:20
  135.3 11.9 %collective-permute-start.21 = (bf16[2,2,2,16,1024]{4,3,2,1,0:T(8,128)(2,1)S(1)}, bf16[2,2,2,16,1024]{4,3,2,1,0:T(8,128)(2,1)}, u32[]{:S(2)}, u32[]{:S(2)}) collective-permute-start(bf16[2,2,2,16,1024]{4,3,2,1,0:T(8,128)(2,1)S(1)} %get-tuple-element.13), channel_id=1, source_target_pairs={{0,64},{16,80},{32,96},{48,112},{64,0},{80,16},{96,32},{112,48},{1... | collective-permute-start | bytes 786440 | tf_op jit(solution)/shard_map/ppermute | solution.py:20
  159.0 11.1 %collective-permute-start.24 = (bf16[2,2,32,1024]{3,2,1,0:T(8,128)(2,1)S(1)}, bf16[2,2,32,1024]{3,2,1,0:T(8,128)(2,1)S(1)}, u32[]{:S(2)}, u32[]{:S(2)}) collective-permute-start(bf16[2,2,32,1024]{3,2,1,0:T(8,128)(2,1)S(1)} %get-tuple-element.40), channel_id=1, source_target_pairs={{0,96},{16,112},{32,0},{48,16},{64,32},{80,48},{96,64},{112,80},{1... | collective-permute-start | bytes 786440 | tf_op jit(solution)/shard_map/ppermute | solution.py:20
  162.0 9.1 %collective-permute-start.25 = (bf16[2,2,32,1024]{3,2,1,0:T(8,128)(2,1)S(1)}, bf16[2,2,32,1024]{3,2,1,0:T(8,128)(2,1)S(1)}, u32[]{:S(2)}, u32[]{:S(2)}) collective-permute-start(bf16[2,2,32,1024]{3,2,1,0:T(8,128)(2,1)S(1)} %get-tuple-element.40), channel_id=1, source_target_pairs={{0,64},{16,80},{32,96},{48,112},{64,0},{80,16},{96,32},{112,48},{1... | collective-permute-start | bytes 786440 | tf_op jit(solution)/shard_map/ppermute | solution.py:20
  162.1 11.5 %collective-permute-start.26 = (bf16[2,2,32,1024]{3,2,1,0:T(8,128)(2,1)S(1)}, bf16[2,2,32,1024]{3,2,1,0:T(8,128)(2,1)S(1)}, u32[]{:S(2)}, u32[]{:S(2)}) collective-permute-start(bf16[2,2,32,1024]{3,2,1,0:T(8,128)(2,1)S(1)} %get-tuple-element.40), channel_id=1, source_target_pairs={{0,32},{16,48},{32,64},{48,80},{64,96},{80,112},{96,0},{112,16},{1... | collective-permute-start | bytes 786440 | tf_op jit(solution)/shard_map/ppermute | solution.py:20
  192.0 22.4 %collective-permute-start.28 = (bf16[2,32,3328]{2,1,0:T(8,128)(2,1)}, bf16[2,32,3328]{2,1,0:T(8,128)(2,1)S(1)}, u32[]{:S(2)}, u32[]{:S(2)}) collective-permute-start(bf16[2,32,3328]{2,1,0:T(8,128)(2,1)} %get-tuple-element.9), channel_id=1, source_target_pairs={{0,4},{1,5},{2,6},{3,7},{4,8},{5,9},{6,10},{7,11},{8,12},{9,13},{1... | collective-permute-start | bytes 1277960 | tf_op jit(solution)/shard_map/ppermute | solution.py:16
  192.2 22.2 %collective-permute-start.29 = (bf16[2,32,3328]{2,1,0:T(8,128)(2,1)}, bf16[2,32,3328]{2,1,0:T(8,128)(2,1)S(1)}, u32[]{:S(2)}, u32[]{:S(2)}) collective-permute-start(bf16[2,32,3328]{2,1,0:T(8,128)(2,1)} %get-tuple-element.11), channel_id=1, source_target_pairs={{0,12},{1,13},{2,14},{3,15},{4,0},{5,1},{6,2},{7,3},{8,4},{9,5},{1... | collective-permute-start | bytes 1277960 | tf_op jit(solution)/shard_map/ppermute | solution.py:16
  195.3 19.2 %collective-permute-start.30 = (bf16[2,32,3328]{2,1,0:T(8,128)(2,1)S(1)}, bf16[2,32,3328]{2,1,0:T(8,128)(2,1)S(1)}, u32[]{:S(2)}, u32[]{:S(2)}) collective-permute-start(bf16[2,32,3328]{2,1,0:T(8,128)(2,1)S(1)} %get-tuple-element.10), channel_id=1, source_target_pairs={{0,8},{1,9},{2,10},{3,11},{4,12},{5,13},{6,14},{7,15},{8,0},{9,1},... | collective-permute-start | bytes 1277960 | tf_op jit(solution)/shard_map/ppermute | solution.py:16
  215.8 8.0 %collective-permute-start.31 = (bf16[2,16,3328]{2,1,0:T(8,128)(2,1)S(1)}, bf16[2,16,3328]{2,1,0:T(8,128)(2,1)S(1)}, u32[]{:S(2)}, u32[]{:S(2)}) collective-permute-start(bf16[2,16,3328]{2,1,0:T(8,128)(2,1)S(1)} %fusion.34), channel_id=1, source_target_pairs={{0,2},{1,3},{2,0},{3,1},{4,6},{5,7},{6,4},{7,5},{8,10},{9,11},{10,... | collective-permute-start | bytes 638984 | tf_op jit(solution)/shard_map/ppermute | solution.py:28
  224.2 7.4 %collective-permute-start.32 = (bf16[2,16,3328]{2,1,0:T(8,128)(2,1)S(1)}, bf16[2,16,3328]{2,1,0:T(8,128)(2,1)S(1)}, u32[]{:S(2)}, u32[]{:S(2)}) collective-permute-start(bf16[2,16,3328]{2,1,0:T(8,128)(2,1)S(1)} %get-tuple-element.44), channel_id=1, source_target_pairs={{0,2},{1,3},{2,0},{3,1},{4,6},{5,7},{6,4},{7,5},{8,10},{9,11},{10,... | collective-permute-start | bytes 638984 | tf_op jit(solution)/shard_map/ppermute | solution.py:28
  231.7 18.1 %collective-permute-start.33 = (bf16[2,2,16,3328]{3,2,1,0:T(8,128)(2,1)S(1)}, bf16[2,2,16,3328]{3,2,1,0:T(8,128)(2,1)S(1)}, u32[]{:S(2)}, u32[]{:S(2)}) collective-permute-start(bf16[2,2,16,3328]{3,2,1,0:T(8,128)(2,1)S(1)} %get-tuple-element.36), channel_id=1, source_target_pairs={{0,12},{1,13},{2,14},{3,15},{4,0},{5,1},{6,2},{7,3},{8,4},{9,5},{1... | collective-permute-start | bytes 1277960 | tf_op jit(solution)/shard_map/ppermute | solution.py:16
  234.4 15.4 %collective-permute-start.34 = (bf16[2,2,16,3328]{3,2,1,0:T(8,128)(2,1)S(1)}, bf16[2,2,16,3328]{3,2,1,0:T(8,128)(2,1)S(1)}, u32[]{:S(2)}, u32[]{:S(2)}) collective-permute-start(bf16[2,2,16,3328]{3,2,1,0:T(8,128)(2,1)S(1)} %get-tuple-element.36), channel_id=1, source_target_pairs={{0,8},{1,9},{2,10},{3,11},{4,12},{5,13},{6,14},{7,15},{8,0},{9,1},... | collective-permute-start | bytes 1277960 | tf_op jit(solution)/shard_map/ppermute | solution.py:16
  234.6 18.8 %collective-permute-start.35 = (bf16[2,2,16,3328]{3,2,1,0:T(8,128)(2,1)S(1)}, bf16[2,2,16,3328]{3,2,1,0:T(8,128)(2,1)S(1)}, u32[]{:S(2)}, u32[]{:S(2)}) collective-permute-start(bf16[2,2,16,3328]{3,2,1,0:T(8,128)(2,1)S(1)} %get-tuple-element.36), channel_id=1, source_target_pairs={{0,4},{1,5},{2,6},{3,7},{4,8},{5,9},{6,10},{7,11},{8,12},{9,13},{1... | collective-permute-start | bytes 1277960 | tf_op jit(solution)/shard_map/ppermute | solution.py:16
  263.4 6.8 %collective-permute-start.37 = (bf16[2,2,1,16,1024]{4,3,1,0,2:T(8,128)(2,1)S(1)}, bf16[2,2,1,16,1024]{4,3,1,0,2:T(8,128)(2,1)S(1)}, u32[]{:S(2)}, u32[]{:S(2)}) collective-permute-start(bf16[2,2,1,16,1024]{4,3,1,0,2:T(8,128)(2,1)S(1)} %get-tuple-element.25), channel_id=1, source_target_pairs={{0,32},{16,48},{32,64},{48,80},{64,96},{80,112},{96,0},{112,16},{1... | collective-permute-start | bytes 393224 | tf_op jit(solution)/shard_map/ppermute | solution.py:20
  263.4 8.8 %collective-permute-start.38 = (bf16[2,2,1,16,1024]{4,3,1,0,2:T(8,128)(2,1)S(1)}, bf16[2,2,1,16,1024]{4,3,1,0,2:T(8,128)(2,1)S(1)}, u32[]{:S(2)}, u32[]{:S(2)}) collective-permute-start(bf16[2,2,1,16,1024]{4,3,1,0,2:T(8,128)(2,1)S(1)} %get-tuple-element.26), channel_id=1, source_target_pairs={{0,96},{16,112},{32,0},{48,16},{64,32},{80,48},{96,64},{112,80},{1... | collective-permute-start | bytes 393224 | tf_op jit(solution)/shard_map/ppermute | solution.py:20
  (28 other events, 273.2 us)
